TPU v7x, 32 devices: a whole 2x2x4 slice. The times are simulated.
32 devices in a mesh: blk: 2 (over y), uly: 4 (over x, core), dp: 4 (over z).
Axes of the slice: x: 2, y: 2, z: 4, core: 2. Of those that a mesh axis runs over, the one named last changes fastest.
Arguments:
- tokens: bfloat16 [1024, 4096], P(('uly', 'dp')), may hold values from -6 to 6
- expert_ids: int32 [1024, 8], P(('uly', 'dp')), may hold values from 0 to 15, all different within a row; in each aligned block of 64 rows (0 to 63, 64 to 127, ...) at most 40 rows name the same one
- route_weight: float32 [1024, 8], P(('uly', 'dp')), may hold values from 0.05 to 0.5
- w_gate: bfloat16 [16, 4096, 1024], P(('uly', 'dp'), None, 'blk'), may hold values from -0.09375 to 0.09375
- w_up: bfloat16 [16, 4096, 1024], P(('uly', 'dp'), None, 'blk'), may hold values from -0.09375 to 0.09375
- w_down: bfloat16 [16, 1024, 4096], P(('uly', 'dp'), 'blk'), may hold values from -0.1875 to 0.1875
Outputs:
- mixed: bfloat16 [1024, 4096], P(('uly', 'dp'), 'blk')
Inputs may be any that keep to these rules, and one draw needn't show every extreme that they name: `expert_ids`: each row names 8 different experts. In each aligned block of 64 rows (the rows of one device) no expert is named by more than 40 rows, and in some block one expert is named by exactly 40 rows.
All inputs are finite; a program needn't handle non-finite values.
Results may differ from a plain program's by a relative error of at most 0.015.
Values may be sent and summed in bfloat16 or wider, within the bound.
A program may use at most 64 MiB of HBM per device.

v0:
```python
import jax
import jax.numpy as jnp
from jax import lax
from jax.sharding import PartitionSpec as P


def routing_tables(expert_ids, route_weight, groups, local_count, capacity):
    tokens_here, picks_count = expert_ids.shape
    experts = groups * local_count
    labels = lax.broadcasted_iota(jnp.int32, (1, 1, experts), 2)
    onehot = (expert_ids[:, :, None] == labels).astype(jnp.int32)
    chosen = jnp.sum(onehot, axis=1)
    before = jnp.cumsum(chosen, axis=0) - chosen
    slot_of = jnp.sum(onehot * before[:, None, :], axis=2)
    places = lax.broadcasted_iota(jnp.int32, (1, 1, capacity), 2)
    slot_hot = (slot_of[:, :, None] == places).astype(jnp.float32)
    expert_hot = onehot.astype(jnp.float32).reshape(tokens_here, picks_count, groups, local_count)
    placing = jnp.einsum("tkgl,tkc->gclt", expert_hot, slot_hot)
    placing = placing.reshape(groups * capacity * local_count, tokens_here)
    mixing = jnp.einsum("tkgl,tkc,tk->tgcl", expert_hot, slot_hot, route_weight)
    mixing = mixing.reshape(tokens_here, groups * capacity * local_count)
    return (placing.astype(jnp.bfloat16), mixing)


def local_slots(tokens, expert_ids, route_weight, w_gate, w_up, w_down):
    ulysses_size = lax.axis_size("uly")
    data_size = lax.axis_size("dp")
    cycle_size = lax.axis_size("blk")
    tokens_here, model_width = tokens.shape
    local_count = w_gate.shape[0]
    hidden_cut = w_gate.shape[2]
    groups = ulysses_size * data_size
    experts = groups * local_count
    picks_count = expert_ids.shape[1]
    capacity = min(tokens_here, max(2, 5 * tokens_here * picks_count // (4 * experts)))
    placing, mixing = routing_tables(expert_ids, route_weight, groups, local_count, capacity)
    slice_width = model_width // cycle_size
    rows_total = groups * capacity
    cycle_index = lax.axis_index("blk")
    own_part = lax.dynamic_slice_in_dim(tokens, cycle_index * slice_width, slice_width, 1)
    outgoing = jnp.dot(placing, own_part, preferred_element_type=jnp.float32).astype(jnp.bfloat16)
    outgoing = outgoing.reshape(ulysses_size, data_size, capacity, local_count, slice_width)
    arrived = lax.all_to_all(
        lax.all_to_all(outgoing, "uly", split_axis=0, concat_axis=0, tiled=True),
        "dp",
        split_axis=1,
        concat_axis=1,
        tiled=True,
    )
    arrived = arrived.reshape(rows_total, local_count, slice_width)
    portion = lax.all_gather(arrived, "blk", axis=2, tiled=True)
    gate_more = jnp.einsum("rlw,lwf->rlf", portion, w_gate, preferred_element_type=jnp.float32)
    up_more = jnp.einsum("rlw,lwf->rlf", portion, w_up, preferred_element_type=jnp.float32)
    hidden = (jax.nn.silu(gate_more) * up_more).astype(jnp.bfloat16)
    resplit = lax.all_to_all(w_down, "blk", split_axis=2, concat_axis=1, tiled=True)
    zero_sum = jnp.zeros((slice_width, rows_total * local_count), jnp.float32)
    total = zero_sum
    portion = lax.all_gather(hidden, "blk", axis=2, tiled=True)
    ranges_count = portion.shape[2] // hidden_cut
    for number in range(ranges_count):
        part_hidden = portion[:, :, number * hidden_cut : (number + 1) * hidden_cut]
        part_rows = lax.dynamic_slice_in_dim(resplit, number * hidden_cut, hidden_cut, 1)
        partial_value = jnp.einsum(
            "lfd,rlf->drl", part_rows, part_hidden, preferred_element_type=jnp.float32
        )
        partial_value = partial_value.reshape(slice_width, rows_total * local_count)
        total = total + partial_value.astype(jnp.bfloat16).astype(jnp.float32)
    returned = total.astype(jnp.bfloat16).reshape(
        slice_width, ulysses_size, data_size, capacity, local_count
    )
    returned_rows = lax.all_to_all(
        lax.all_to_all(returned, "uly", split_axis=1, concat_axis=1, tiled=True),
        "dp",
        split_axis=2,
        concat_axis=2,
        tiled=True,
    )
    returned_rows = returned_rows.reshape(slice_width, rows_total * local_count).astype(jnp.float32)
    mixed = lax.dot_general(
        mixing, returned_rows, (((1,), (1,)), ((), ())), precision=lax.Precision.HIGHEST
    )
    return mixed.astype(jnp.bfloat16)


def local_dense(tokens, expert_ids, route_weight, w_gate, w_up, w_down):
    data_size = lax.axis_size("dp")
    local_count = w_gate.shape[0]
    groups = lax.axis_size("uly") * data_size
    experts = groups * local_count
    labels = lax.broadcasted_iota(jnp.int32, (1, 1, experts), 2)
    scaled = jnp.sum(
        jnp.where(expert_ids[:, :, None] == labels, route_weight[:, :, None], 0.0), axis=1
    )
    everyone = lax.all_gather(tokens, ("uly", "dp"), axis=0, tiled=True)
    shares = lax.all_gather(scaled, ("uly", "dp"), axis=0, tiled=True)
    first = (lax.axis_index("uly") * data_size + lax.axis_index("dp")) * local_count
    total = None
    for number in range(local_count):
        share = lax.dynamic_slice_in_dim(shares, first + number, 1, 1)
        gate = jnp.dot(everyone, w_gate[number], preferred_element_type=jnp.float32)
        up = jnp.dot(everyone, w_up[number], preferred_element_type=jnp.float32)
        hidden = (jax.nn.silu(gate) * up * share).astype(jnp.bfloat16)
        part = jnp.dot(hidden, w_down[number], preferred_element_type=jnp.float32)
        total = part if total is None else total + part
    halves = lax.psum_scatter(total.astype(jnp.bfloat16), "blk", scatter_dimension=1, tiled=True)
    return lax.psum_scatter(halves, ("uly", "dp"), scatter_dimension=0, tiled=True)


def solution(mesh):
    groups = mesh.shape["uly"] * mesh.shape["dp"]
    return jax.shard_map(
        local_dense if groups <= 16 else local_slots,
        mesh=mesh,
        in_specs=(
            P(("uly", "dp"), None),
            P(("uly", "dp"), None),
            P(("uly", "dp"), None),
            P(("uly", "dp"), None, "blk"),
            P(("uly", "dp"), None, "blk"),
            P(("uly", "dp"), "blk", None),
        ),
        out_specs=P(("uly", "dp"), "blk"),
        check_vma=False,
    )
```

profile of v0, /device:TPU:0, one launch (start us, length us, event | category | flops | bytes accessed | tf_op | source)
XLA Modules:
  0.0 293.6 jit_solution(17746111028157414352)
XLA Ops:
  6.5 0.0 all-gather.3.cloned.1.call-start
  6.5 0.7 all-gather.3.cloned.1.call-update
  7.3 0.0 reduce-scatter.3.cloned.1.call-start
  7.3 0.7 select_reduce_fusion
  8.0 36.9 %all-gather = f32[16,64,16]{1,2,0:T(8,128)S(1)} all-gather(f32[1,64,16]{1,2,0:T(8,128)S(1)} %bitcast.19), channel_id=1, replica_groups=mesh['blk'=2,'uly'=4,'dp'=4] {'uly','dp'}, dimensions={0}, use_global_device_ids=true | all-gather | bytes 69632 | tf_op jit(solution)/shard_map/all_gather | solution.py:95
  45.0 0.1 reshape.3
  45.1 43.0 %all-gather.3.cloned.1.call-done = bf16[1024,4096]{1,0:T(8,128)(2,1)} async-done(((bf16[64,4096]{1,0:T(8,128)(2,1)}), bf16[1024,4096]{1,0:T(8,128)(2,1)}) %all-gather.3.cloned.1.call-update) | async-done | bytes 8388624 | tf_op jit(solution)/shard_map/all_gather | solution.py:94
  88.2 8.1 %fusion.3 = f32[1024,512]{1,0:T(8,128)S(1)} fusion(bf16[1024,4096]{1,0:T(8,128)(2,1)} %all-gather.3.cloned.1.call-done, bf16[1,4096,512]{2,1,0:T(8,128)(2,1)} %param.9), kind=kOutput, calls=%fused_computation.4 | convolution fusion | flops 4294967296 | bytes 14680064 | tf_op jit(solution)/shard_map/dot_general | solution.py:100
  96.3 16.0 %convolution_convert_fusion = bf16[1024,4096]{1,0:T(8,128)(2,1)} fusion(bf16[1,512,4096]{2,1,0:T(8,128)(2,1)} %param.11, f32[1024,512]{1,0:T(8,128)S(1)} %fusion.3, bf16[1024,4096]{1,0:T(8,128)(2,1)} %all-gather.3.cloned.1.call-done, bf16[1,4096,512]{2,1,0:T(8,128)(2,1)} %param.10, f32[1024]{0:T(1024)S(1)} %bitcast.20), kind=kOutput, calls=%fused_computation | convolution fusion | flops 8597798912 | bytes 27267072 | tf_op jit(solution)/shard_map/dot_general | solution.py:103
  112.3 0.0 reduce-scatter.3.cloned.1.call-update
  112.3 0.0 reduce-scatter.5.cloned.1.call-start
  112.4 98.0 %reduce-scatter.3.cloned.1.call-done = bf16[1024,2048]{1,0:T(8,128)(2,1)} async-done(((bf16[1024,4096]{1,0:T(8,128)(2,1)}), bf16[1024,2048]{1,0:T(8,128)(2,1)}) %reduce-scatter.3.cloned.1.call-update) | async-done | bytes 4194320 | tf_op jit(solution)/shard_map/reduce_scatter | solution.py:105
  210.4 0.0 reduce-scatter.5.cloned.1.call-update
  210.4 76.7 %reduce-scatter.5.cloned.1.call-done = bf16[64,2048]{1,0:T(8,128)(2,1)} async-done(((bf16[1024,2048]{1,0:T(8,128)(2,1)}), bf16[64,2048]{1,0:T(8,128)(2,1)}) %reduce-scatter.5.cloned.1.call-update) | async-done | bytes 262160 | tf_op jit(solution)/shard_map/reduce_scatter | solution.py:106
  (2 shorter events, 0.1 us)
Async XLA Ops:
  6.5 81.6 %all-gather.3.cloned.1.call-start = ((), (), s32[]{:S(2)}) async-start(), calls=%async_computation.2 | async-start | bytes 8912896 | tf_op jit(solution)/shard_map/all_gather | solution.py:94
  7.3 203.1 %reduce-scatter.3.cloned.1.call-start = ((), (), s32[]{:S(2)}) async-start(), calls=%async_computation.3 | async-start | bytes 12582912 | tf_op jit(solution)/shard_map/reduce_scatter | solution.py:105
  112.3 174.8 %reduce-scatter.5.cloned.1.call-start = ((), (), s32[]{:S(2)}) async-start(), calls=%async_computation.4 | async-start | bytes 4456448 | tf_op jit(solution)/shard_map/reduce_scatter | solution.py:106
Sparse Core Ops, SparseCore 0:
  9.5 78.5 all-gather.2
  112.4 97.8 reduce-scatter.2
  214.2 72.7 reduce-scatter.4
where the time goes:
time: 294 us
  waiting for transfers between devices  218 us (74%)
  blocking collectives  36.9 us (13%)
  matrix products  24.1 us (8%)
  between operations  13.1 us (4%)
    reduce_scatter x1, waiting for transfers between devices, local_dense(): lax.psum_scatter(total.astype(jnp.bfloat16), 'blk', scatter_dimension=1,...  98 us
    reduce_scatter x1, waiting for transfers between devices, local_dense(): lax.psum_scatter(halves, ('uly', 'dp'), scatter_dimension=0, tiled=True)  76.7 us
    all_gather x1, waiting for transfers between devices, local_dense(): everyone = lax.all_gather(tokens, ('uly', 'dp'), axis=0, tiled=True)  43 us
    all_gather x1, blocking collectives, local_dense(): shares = lax.all_gather(scaled, ('uly', 'dp'), axis=0, tiled=True)  36.9 us
    dot_general x1, matrix products, local_dense(): part = jnp.dot(hidden, w_down[number], preferred_element_type=jnp.float32)  16 us
    dot_general x1, matrix products, local_dense(): gate = jnp.dot(everyone, w_gate[number], preferred_element_type=jnp.float32)  8.14 us
  transfers between devices with their start and end apart: 3, of which 3 were waited for; matrix products, arithmetic and copies ran while one was open for 0% of the time, Pallas kernels for 0%

commit v1 on v0

--- a/solution.py
+++ b/solution.py
@@ -91,8 +91,13 @@
     scaled = jnp.sum(
         jnp.where(expert_ids[:, :, None] == labels, route_weight[:, :, None], 0.0), axis=1
     )
-    everyone = lax.all_gather(tokens, ("uly", "dp"), axis=0, tiled=True)
-    shares = lax.all_gather(scaled, ("uly", "dp"), axis=0, tiled=True)
+    everyone, shares = jnp.split(
+        lax.all_gather(
+            jnp.concatenate([tokens, scaled], axis=1), ("uly", "dp"), axis=0, tiled=True
+        ),
+        [tokens.shape[1]],
+        axis=1,
+    )
     first = (lax.axis_index("uly") * data_size + lax.axis_index("dp")) * local_count
     total = None
     for number in range(local_count):

time: 294 us -> 320 us (1.088)
  waiting for transfers between devices: 218 us -> 275 us
  blocking collectives: 36.9 us -> 0 us
    all_gather x1, waiting for transfers between devices: 43 us -> 99 us  [local_dense(): lax.all_gather(jnp.concatenate([tokens, scaled], axis=1), ('uly', 'dp'),...]
    all_gather x1 -> x0, blocking collectives: 36.9 us -> none  [local_dense(): shares = lax.all_gather(scaled, ('uly', 'dp'), axis=0, tiled=True)]
where the time goes in v1:
time: 320 us; the launch traced here: 319 us
  waiting for transfers between devices  275 us (86%)
  matrix products  26.5 us (8%)
  between operations  13.1 us (4%)
    reduce_scatter x1, waiting for transfers between devices, local_dense(): lax.psum_scatter(total.astype(jnp.bfloat16), 'blk', scatter_dimension=1,...  99.4 us
    all_gather x1, waiting for transfers between devices, local_dense(): lax.all_gather(jnp.concatenate([tokens, scaled], axis=1), ('uly', 'dp'),...  99 us
    reduce_scatter x1, waiting for transfers between devices, local_dense(): lax.psum_scatter(halves, ('uly', 'dp'), scatter_dimension=0, tiled=True)  76.7 us
    dot_general x1, matrix products, local_dense(): part = jnp.dot(hidden, w_down[number], preferred_element_type=jnp.float32)  17.1 us
    dot_general x1, matrix products, local_dense(): gate = jnp.dot(everyone, w_gate[number], preferred_element_type=jnp.float32)  9.31 us
  transfers between devices with their start and end apart: 3, of which 3 were waited for; matrix products, arithmetic and copies ran while one was open for 0% of the time, Pallas kernels for 0%

profile of v1, /device:TPU:0, one launch (start us, length us, event | category | flops | bytes accessed | tf_op | source)
XLA Modules:
  0.0 319.3 jit_solution(12720733927891132682)
XLA Ops:
  6.5 0.0 all-gather.2.cloned.1.call-start
  6.5 0.7 select_reduce_fusion
  7.3 0.1 copy.11
  7.3 1.1 convert_element_type.9
  8.5 1.1 pad_maximum_fusion
  9.5 0.0 all-gather.2.cloned.1.call-update
  9.5 0.0 reduce-scatter.3.cloned.1.call-start
  9.6 99.0 %all-gather.2.cloned.1.call-done = f32[1024,4112]{1,0:T(8,128)} async-done(((f32[64,4112]{1,0:T(8,128)}), f32[1024,4112]{1,0:T(8,128)}) %all-gather.2.cloned.1.call-update) | async-done | bytes 16842768 | tf_op jit(solution)/shard_map/all_gather | solution.py:95
  108.7 1.1 split.9
  109.7 0.4 dynamic-slice_reduce_fusion
  110.1 9.3 %fusion.2 = f32[1024,512]{1,0:T(8,128)S(1)} fusion(f32[1024,4112]{1,0:T(8,128)} %all-gather.2.cloned.1.call-done, bf16[1,4096,512]{2,1,0:T(8,128)(2,1)} %param.9), kind=kOutput, calls=%fused_computation.2 | convolution fusion | flops 4294967296 | bytes 14680064 | tf_op jit(solution)/shard_map/dot_general | solution.py:105
  119.4 17.1 %convolution_convert_fusion = bf16[1024,4096]{1,0:T(8,128)(2,1)} fusion(bf16[1,512,4096]{2,1,0:T(8,128)(2,1)} %param.11, f32[1024,512]{1,0:T(8,128)S(1)} %fusion.2, bf16[1,4096,512]{2,1,0:T(8,128)(2,1)} %param.10, f32[1024,4112]{1,0:T(8,128)} %all-gather.2.cloned.1.call-done, f32[1024]{0:T(1024)S(1)} %dynamic-slice_reduce_fusion), kind=kOutput, calls=%fused_computation.4 | convolution fusion | flops 8597798912 | bytes 27267072 | tf_op jit(solution)/shard_map/dot_general | solution.py:108
  136.6 0.0 reduce-scatter.3.cloned.1.call-update
  136.6 0.0 reduce-scatter.5.cloned.1.call-start
  136.6 99.4 %reduce-scatter.3.cloned.1.call-done = bf16[1024,2048]{1,0:T(8,128)(2,1)} async-done(((bf16[1024,4096]{1,0:T(8,128)(2,1)}), bf16[1024,2048]{1,0:T(8,128)(2,1)}) %reduce-scatter.3.cloned.1.call-update) | async-done | bytes 4194320 | tf_op jit(solution)/shard_map/reduce_scatter | solution.py:110
  236.1 0.0 reduce-scatter.5.cloned.1.call-update
  236.1 76.7 %reduce-scatter.5.cloned.1.call-done = bf16[64,2048]{1,0:T(8,128)(2,1)} async-done(((bf16[1024,2048]{1,0:T(8,128)(2,1)}), bf16[64,2048]{1,0:T(8,128)(2,1)}) %reduce-scatter.5.cloned.1.call-update) | async-done | bytes 262160 | tf_op jit(solution)/shard_map/reduce_scatter | solution.py:111
Async XLA Ops:
  6.5 102.1 %all-gather.2.cloned.1.call-start = ((), (), s32[]{:S(2)}) async-start(), calls=%async_computation.2 | async-start | bytes 18382848 | tf_op jit(solution)/shard_map/all_gather | solution.py:95
  9.5 226.5 %reduce-scatter.3.cloned.1.call-start = ((), (), s32[]{:S(2)}) async-start(), calls=%async_computation.3 | async-start | bytes 12582912 | tf_op jit(solution)/shard_map/reduce_scatter | solution.py:110
  136.6 176.2 %reduce-scatter.5.cloned.1.call-start = ((), (), s32[]{:S(2)}) async-start(), calls=%async_computation.4 | async-start | bytes 4456448 | tf_op jit(solution)/shard_map/reduce_scatter | solution.py:111
Sparse Core Ops, SparseCore 0:
  9.7 98.9 all-gather.1
  136.7 99.2 reduce-scatter.2
  239.9 72.7 reduce-scatter.4
